TPU v7x, 32 devices: a whole 2x2x4 slice. The times are simulated.
32 devices in a mesh: ma: 4 (over x, core), ell: 8 (over z, y).
Axes of the slice: x: 2, y: 2, z: 4, core: 2. Of those that a mesh axis runs over, the one named last changes fastest.
Arguments:
- legendre: bfloat16 [3, 2048, 2, 4096], P(None, 'ma', None, 'ell'), may hold values from -6 to 6
- harmonics: bfloat16 [2048, 3, 2, 4, 4096], P('ma', None, None, None, 'ell'), may hold values from -0.0014648438 to 0.0014648438
- slot_orders: int32 [2048], replicated, may hold values from 0 to 2047, each once
- cycle_index: int32 [2], replicated, may hold values from 2048 to 4095
Outputs:
- maps: float32 [4, 3, 4, 8192], P('ma', None, None, 'ell')
Inputs may be any that keep to these rules, and one draw needn't show every extreme that they name: `slot_orders`: every number from 0 to 2047 appears once.
All inputs are finite; a program needn't handle non-finite values.
Results may differ from a plain program's by a relative error of at most 0.0003.
Values sent between devices are 32-bit elements; how exact they have to be, the bound alone decides.
A program may use at most 128 MiB of HBM per device.

v0:
```python
import math

import jax
import jax.numpy as jnp
from jax import lax
from jax.sharding import PartitionSpec as P


def column_weights(lower_order, first_column, columns_count, full_width):
    columns = first_column + jnp.arange(columns_count, dtype=jnp.int32)
    boundary = (full_width - 1 - lower_order)[:, None]
    lower_part = (columns[None, :] < boundary).astype(jnp.float32)
    upper_part = ((columns[None, :] >= boundary) & (columns[None, :] < full_width - 1)).astype(
        jnp.float32
    )
    lower_sign = (1 - 2 * (columns[None, :] % 2)).astype(jnp.float32)
    upper_sign = (1 - 2 * ((columns[None, :] + 1 + lower_order[:, None]) % 2)).astype(jnp.float32)
    return jnp.stack(
        [lower_part, lower_part * lower_sign, upper_part, upper_part * upper_sign], axis=1
    )


def spin_fields(plain, plus, minus):
    hemisphere = jnp.array([1.0, -1.0], jnp.float32).reshape(1, 1, 1, 2, 1, 1, 1)
    minus = minus * hemisphere
    temp_real = plain[:, :, :, :, 0]
    temp_imag = plain[:, :, :, :, 1]
    eplus_real = plus[:, :, :, :, 0, 0]
    eplus_imag = plus[:, :, :, :, 0, 1]
    bplus_real = plus[:, :, :, :, 1, 0]
    bplus_imag = plus[:, :, :, :, 1, 1]
    eminus_real = minus[:, :, :, :, 0, 0]
    eminus_imag = minus[:, :, :, :, 0, 1]
    bminus_real = minus[:, :, :, :, 1, 0]
    bminus_imag = minus[:, :, :, :, 1, 1]
    stokes_q_real = -(eplus_real - bminus_imag)
    stokes_q_imag = -(eplus_imag + bminus_real)
    stokes_u_real = -(bplus_real + eminus_imag)
    stokes_u_imag = -(bplus_imag - eminus_real)
    return jnp.stack(
        [
            jnp.stack([temp_real, temp_imag]),
            jnp.stack([stokes_q_real, stokes_q_imag]),
            jnp.stack([stokes_u_real, stokes_u_imag]),
        ]
    )


def place_orders(cycle_orders, lower_all):
    highest = lax.Precision.HIGHEST
    half = lower_all.shape[0]
    width = min(512, half)
    pieces = []
    for start in range(0, half, width):
        targets = start + jnp.arange(width, dtype=jnp.int32)
        onehot = (lower_all[:, None] == targets[None, :]).astype(jnp.float32)
        pieces.append(jnp.einsum("abcdes,sm->abcdem", cycle_orders, onehot, precision=highest))
    placed = jnp.concatenate(pieces, axis=-1)
    return jnp.concatenate([placed[..., 0, :], jnp.flip(placed[..., 1, :], axis=-1)], axis=-1)


def cycle_synthesis(coeff, shift, first_group, group_count):
    highest = lax.Precision.HIGHEST
    cycles_count = coeff.shape[0]
    components = coeff.shape[3]
    orders_count = coeff.shape[-1]
    pixels = 2 * orders_count
    outer = pixels // 128
    groups = orders_count // 128
    orders = jnp.arange(orders_count, dtype=jnp.int32)
    phase = (orders[None, :] * shift[:, None] % (2 * pixels)).astype(jnp.float32) * (
        math.pi / pixels
    )
    factor = jnp.where(orders == 0, 1.0, 2.0).astype(jnp.float32)
    cosine = (jnp.cos(phase) * factor)[:, None, None, :]
    sine = (jnp.sin(phase) * factor)[:, None, None, :]
    real_part = coeff[:, :, 0]
    imag_part = coeff[:, :, 1]
    shifted_real = (real_part * cosine - imag_part * sine).reshape(
        cycles_count, 3, components, groups, 128
    )
    shifted_imag = (real_part * sine + imag_part * cosine).reshape(
        cycles_count, 3, components, groups, 128
    )
    group_ids = jnp.arange(groups, dtype=jnp.int32)
    outer_ids = jnp.arange(outer, dtype=jnp.int32)
    inner_ids = jnp.arange(128, dtype=jnp.int32)
    angle_one = (group_ids[:, None] * outer_ids[None, :] % outer).astype(jnp.float32) * (
        2.0 * math.pi / outer
    )
    cos_one = jnp.cos(angle_one)
    sin_one = jnp.sin(angle_one)
    first_real = jnp.einsum(
        "xyzab,ak->xyzkb", shifted_real, cos_one, precision=highest
    ) - jnp.einsum("xyzab,ak->xyzkb", shifted_imag, sin_one, precision=highest)
    first_imag = jnp.einsum(
        "xyzab,ak->xyzkb", shifted_real, sin_one, precision=highest
    ) + jnp.einsum("xyzab,ak->xyzkb", shifted_imag, cos_one, precision=highest)
    angle_two = (outer_ids[:, None] * inner_ids[None, :] % pixels).astype(jnp.float32) * (
        2.0 * math.pi / pixels
    )
    cos_two = jnp.cos(angle_two)
    sin_two = jnp.sin(angle_two)
    twist_real = first_real * cos_two - first_imag * sin_two
    twist_imag = first_real * sin_two + first_imag * cos_two
    local_ids = first_group + jnp.arange(group_count, dtype=jnp.int32)
    angle_three = (inner_ids[:, None] * local_ids[None, :] % 128).astype(jnp.float32) * (
        2.0 * math.pi / 128
    )
    cos_three = jnp.cos(angle_three)
    sin_three = jnp.sin(angle_three)
    result = jnp.einsum("xyzkb,bq->xyzqk", twist_real, cos_three, precision=highest) - jnp.einsum(
        "xyzkb,bq->xyzqk", twist_imag, sin_three, precision=highest
    )
    return result.reshape(cycles_count, 3, components, group_count * outer)


def body(legendre, harmonics, slot_orders, cycle_index):
    ell_count = lax.axis_size("ell")
    slots_here = harmonics.shape[0]
    columns_here = harmonics.shape[-1]
    components = harmonics.shape[3]
    full_width = 2 * slot_orders.shape[0]
    pairs = cycle_index.shape[0]
    lower_here = lax.dynamic_slice_in_dim(
        slot_orders, lax.axis_index("ma") * slots_here, slots_here
    )
    weights = column_weights(
        lower_here, lax.axis_index("ell") * columns_here, columns_here, full_width
    ).astype(jnp.bfloat16)
    packed = harmonics[:, None] * weights[:, :, None, None, None, :]
    plain = jnp.einsum(
        "srj,sqpcj->srqpc", legendre[0], packed[:, :, 0], preferred_element_type=jnp.float32
    )
    plus = jnp.einsum(
        "srj,sqkpcj->srqkpc", legendre[1], packed[:, :, 1:3], preferred_element_type=jnp.float32
    )
    minus = jnp.einsum(
        "srj,sqkpcj->srqkpc", legendre[2], packed[:, :, 1:3], preferred_element_type=jnp.float32
    )
    plain = plain.reshape(slots_here, pairs, 2, 2, 2, components)
    plus = plus.reshape(slots_here, pairs, 2, 2, 2, 2, components)
    minus = minus.reshape(slots_here, pairs, 2, 2, 2, 2, components)
    fields = spin_fields(plain, plus, minus)
    cycle_sums = fields.transpose(5, 3, 0, 1, 6, 4, 2).reshape(
        2 * pairs, 3, 2, components, 2, slots_here
    )
    summed = lax.psum(cycle_sums, "ell")
    cycle_orders = lax.all_to_all(summed, "ma", split_axis=0, concat_axis=5, tiled=True)
    slot_ids = jnp.arange(slot_orders.shape[0], dtype=jnp.int32)
    lower_all = slot_orders[slot_ids]
    coeff = place_orders(cycle_orders, lower_all)
    cycles_here = cycle_orders.shape[0]
    cycle_ids = lax.axis_index("ma") * cycles_here + jnp.arange(cycles_here, dtype=jnp.int32)
    shift = cycle_index[cycle_ids % pairs] % 2
    per_device = 128 // ell_count
    return cycle_synthesis(coeff, shift, lax.axis_index("ell") * per_device, per_device)


def solution(mesh):
    return jax.shard_map(
        body,
        mesh=mesh,
        in_specs=(P(None, "ma", None, "ell"), P("ma", None, None, None, "ell"), P(), P()),
        out_specs=P("ma", None, None, "ell"),
        check_vma=False,
    )
```

profile of v0, /device:TPU:0, one launch (start us, length us, event | category | flops | bytes accessed | tf_op | source)
XLA Modules:
  0.0 589.4 jit_solution(13482630592718310034)
XLA Ops:
  7.3 2.6 fusion.48
  10.0 1.7 fusion.46
  11.7 6.8 %fusion.45 = bf16[512,1,512]{2,1,0:T(2,128)(2,1)S(1)} fusion(pred[512]{0:T(512)(128)(4,1)S(1)} %fusion.124, s32[512]{0:T(512)S(1)} %get-tuple-element.36, s32[512]{0:T(512)S(1)} %get-tuple-element.35, s32[512]{0:T(512)S(1)} %get-tuple-element.17, s32[512]{0:T(512)S(1)} %get-tuple-element.16), kind=kLoop, calls=%fused_computation.50 | loop fusion | flops 4980736 | bytes 532992 | tf_op jit(solution)/shard_map/convert.3
  18.4 4.9 pad_maximum_fusion
  23.3 41.5 %broadcast_multiply_fusion = bf16[512,4,3,2,4,512]{5,4,3,1,0,2:T(4,128)(2,1)} fusion(bf16[512,4,512]{2,1,0:T(4,128)(2,1)S(1)} %pad_maximum_fusion, bf16[512,3,2,4,512]{4,3,2,1,0:T(4,128)(2,1)} %param.6), kind=kLoop, calls=%fused_computation.5 | loop fusion | flops 100663296 | bytes 65011712 | tf_op jit(solution)/shard_map/mul | solution.py:131
  64.8 151.4 %fusion.2 = f32[512,4,2,2,4,2]{4,5,3,2,1,0:T(2,128)S(1)} fusion(bf16[3,512,2,512]{3,2,1,0:T(2,128)(2,1)} %param.5, bf16[512,4,3,2,4,512]{5,4,3,1,0,2:T(4,128)(2,1)} %broadcast_multiply_fusion), kind=kOutput, calls=%fused_computation.3 | convolution fusion | flops 67108864 | bytes 34865152 | tf_op jit(solution)/shard_map/srj,sqkpcj->srqkpc/dot_general | solution.py:135
  216.2 151.7 %fusion = f32[512,4,2,2,4,2]{4,5,3,2,1,0:T(2,128)} fusion(bf16[3,512,2,512]{3,2,1,0:T(2,128)(2,1)} %param.5, bf16[512,4,3,2,4,512]{5,4,3,1,0,2:T(4,128)(2,1)} %broadcast_multiply_fusion), kind=kOutput, calls=%fused_computation.1 | convolution fusion | flops 67108864 | bytes 34865152 | tf_op jit(solution)/shard_map/srj,sqkpcj->srqkpc/dot_general | solution.py:138
  367.9 77.4 %fusion.4 = f32[512,4,2,4,2]{3,4,2,1,0:T(2,128)} fusion(bf16[512,4,3,2,4,512]{5,4,3,1,0,2:T(4,128)(2,1)} %broadcast_multiply_fusion, bf16[3,512,2,512]{3,2,1,0:T(2,128)(2,1)} %param.5), kind=kOutput, calls=%fused_computation.7 | convolution fusion | flops 33554432 | bytes 17956864 | tf_op jit(solution)/shard_map/srj,sqpcj->srqpc/dot_general | solution.py:132
  445.3 5.4 fusion.149
  450.8 2.7 copy.54
  453.5 10.4 %copy.34 = f32[512,2,2,2,2,2,4]{0,6,3,2,1,5,4:T(4,128)S(1)} copy(f32[512,2,2,2,2,2,4]{6,1,5,4,3,2,0:T(2,128)} %bitcast.150) | data formatting | bytes 524288 | tf_op jit(solution)/shard_map/reshape | solution.py:143
  463.8 2.7 copy.57
  466.5 2.7 copy.56
  470.8 5.0 fusion.150
  475.8 2.7 copy.53
  478.5 1.8 copy.52
  484.4 11.8 %gather_fusion = s32[2048]{0:T(1024)S(1)} fusion(s32[2048]{0:T(1024)S(1)} %copy-done, s32[2048]{0:T(1024)S(1)} %iota_clamp_fusion), kind=kCustom, calls=%fused_computation | custom fusion | bytes 24576 | tf_op jit(solution)/shard_map/gather | solution.py:151
  496.2 60.0 %all-reduce.2.cloned.1.call-done = f32[4,3,2,4,2,512]{5,3,4,2,1,0:T(4,128)} async-done(((f32[4,3,2,4,2,512]{5,3,4,2,1,0:T(4,128)}), f32[4,3,2,4,2,512]{5,3,4,2,1,0:T(4,128)}) %all-reduce.2.cloned.1.call-update) | async-done | bytes 393232 | tf_op jit(solution)/shard_map/psum | solution.py:148
  556.2 3.5 all-to-all-start
  560.0 7.1 %all-to-all-done = f32[4,3,2,4,2,512]{5,3,4,2,1,0:T(4,128)S(1)} async-done(((f32[4,3,2,4,2,512]{5,3,4,2,1,0:T(4,128)}), f32[4,3,2,4,2,512]{5,3,4,2,1,0:T(4,128)S(1)}, u32[]{:S(2)}, u32[]{:S(2)}) %all-to-all-start) | async-done | bytes 393248 | tf_op jit(solution)/shard_map/all_to_all | solution.py:149
  567.7 1.8 fusion.37
  569.5 1.7 fusion.34
  571.2 1.7 fusion.31
  572.9 1.7 fusion.28
  (42 shorter events, 12.5 us)
Async XLA Ops:
  6.5 549.7 %all-reduce.2.cloned.1.call-start = ((), (), s32[]{:S(2)}) async-start(), calls=%async_computation.1 | async-start | bytes 786432 | tf_op jit(solution)/shard_map/psum | solution.py:148
  475.8 4.5 copy-start.1
  475.8 5.8 copy-start.2
  475.8 8.6 %copy-start = (s32[2048]{0:T(1024)S(1)}, s32[2048]{0:T(1024)}, u32[]{:S(2)}) copy-start(s32[2048]{0:T(1024)} %param.7) | copy-start | bytes 24580
  556.2 10.8 %all-to-all-start = ((f32[4,3,2,4,2,512]{5,3,4,2,1,0:T(4,128)}), f32[4,3,2,4,2,512]{5,3,4,2,1,0:T(4,128)S(1)}, u32[]{:S(2)}, u32[]{:S(2)}) async-start(f32[4,3,2,4,2,512]{5,3,4,2,1,0:T(4,128)} %all-reduce.2.cloned.1.call-done), calls=%async_computation | async-start | bytes 786432 | tf_op jit(solution)/shard_map/all_to_all | solution.py:149
Sparse Core Ops, SparseCore 0:
  481.7 74.4 all-reduce.1
where the time goes:
time: 595 us; the launch traced here: 589 us
  matrix products  392 us (66%)
  waiting for transfers between devices  67.2 us (11%)
  other arithmetic  59.1 us (10%)
  local copies, waits for them, and re-layouts  51.4 us (9%)
  between operations  16.2 us (3%)
    dot_general x1, matrix products, body(): jnp.einsum('srj,sqkpcj->srqkpc', legendre[2], packed[:, :, 1:3], preferre...  152 us
    dot_general x1, matrix products, body(): jnp.einsum('srj,sqkpcj->srqkpc', legendre[1], packed[:, :, 1:3], preferre...  151 us
    dot_general x1, matrix products, body(): jnp.einsum('srj,sqpcj->srqpc', legendre[0], packed[:, :, 0], preferred_el...  77.4 us
    psum x1, waiting for transfers between devices, body(): summed = lax.psum(cycle_sums, 'ell')  60 us
    mul x1, other arithmetic, body(): packed = harmonics[:, None] * weights[:, :, None, None, None, :]  41.5 us
    unnamed x12, local copies, waits for them, and re-layouts  14.2 us
  transfers between devices with their start and end apart: 2, of which 2 were waited for; matrix products, arithmetic and copies ran while one was open for 2% of the time, Pallas kernels for 0%

commit v1 on v0

--- a/solution.py
+++ b/solution.py
@@ -1,8 +1,12 @@
+import functools
 import math
 
 import jax
 import jax.numpy as jnp
+import numpy as np
 from jax import lax
+from jax.experimental import pallas as pl
+from jax.experimental.pallas import tpu as pltpu
 from jax.sharding import PartitionSpec as P
 
 
@@ -115,7 +119,7 @@
     return result.reshape(cycles_count, 3, components, group_count * outer)
 
 
-def body(legendre, harmonics, slot_orders, cycle_index):
+def general_body(legendre, harmonics, slot_orders, cycle_index):
     ell_count = lax.axis_size("ell")
     slots_here = harmonics.shape[0]
     columns_here = harmonics.shape[-1]
@@ -157,6 +161,327 @@
     return cycle_synthesis(coeff, shift, lax.axis_index("ell") * per_device, per_device)
 
 
+LANES = 128
+NT = (((1,), (1,)), ((), ()))
+
+
+def rotate_sums(group, lane_tile, sub_pair):
+    turned = None
+    for step in range(4):
+        mixed = group[step]
+        for tile in range(1, 4):
+            mixed = jnp.where(sub_pair == tile, group[(tile + step) % 4], mixed)
+        if step == 0:
+            turned = mixed
+        else:
+            mixed = pltpu.roll(mixed, 2 * step, 0)
+            turned = jnp.where((sub_pair - lane_tile) % 4 == step, mixed, turned)
+    return turned
+
+
+def sums_kernel(full_width, start_ref, orders_ref, table_ref, packed_ref, out_ref, weight_ref, part_ref):
+    step = pl.program_id(0)
+    slots = orders_ref.shape[0]
+    quads = slots // 4
+    all_quads = pl.num_programs(0) * quads
+    rows = slots * 8
+    lower = jnp.broadcast_to(orders_ref[...][:, None, :], (slots, 8, LANES)).reshape(rows, LANES)
+    row = lax.broadcasted_iota(jnp.int32, (rows, LANES), 0)
+    lane = lax.broadcasted_iota(jnp.int32, (rows, LANES), 1)
+    column = start_ref[0] + ((row % 8) // 2) * LANES + lane
+    is_lower = column < full_width - 1 - lower
+    is_upper = jnp.logical_and(jnp.logical_not(is_lower), column < full_width - 1)
+    lower_sign = (1 - 2 * (column % 2)).astype(jnp.float32)
+    upper_sign = (1 - 2 * ((column + 1 + lower) % 2)).astype(jnp.float32)
+    lower_part = jnp.where(is_lower, 1.0, 0.0)
+    upper_part = jnp.where(is_upper, 1.0, 0.0)
+    weight_ref[0] = lower_part.astype(jnp.bfloat16)
+    weight_ref[1] = (lower_part * lower_sign).astype(jnp.bfloat16)
+    weight_ref[2] = upper_part.astype(jnp.bfloat16)
+    weight_ref[3] = (upper_part * upper_sign).astype(jnp.bfloat16)
+
+    sub_pair = lax.broadcasted_iota(jnp.int32, (8, LANES), 0) // 2
+    lane8 = lax.broadcasted_iota(jnp.int32, (8, LANES), 1)
+    lane_tile = (lane8 % 16) // 4
+
+    def one_quad(quad, carry):
+        base = pl.multiple_of(quad * 32, 32)
+        weights = [weight_ref[q, pl.ds(base, 32), :] for q in range(4)]
+        tables = [table_ref[t, pl.ds(base, 32), :] for t in range(3)]
+        first = pl.multiple_of(quad * 384, 32)
+        where_to = pl.multiple_of((step * quads + quad) * 8, 8)
+        left = jnp.concatenate([tables[0] * w for w in weights], axis=0)
+        right = jnp.concatenate(
+            [packed_ref[pl.ds(first + 96 * g, 32), :] for g in range(4)], axis=0
+        )
+        product = lax.dot_general(left, right, NT, preferred_element_type=jnp.float32)
+        group = []
+        for q in range(4):
+            chosen = product[q * 32 : q * 32 + 8]
+            for g in range(1, 4):
+                chosen = jnp.where(
+                    lane8 // 32 == g, product[q * 32 + g * 8 : q * 32 + g * 8 + 8], chosen
+                )
+            group.append(chosen)
+        part_ref[0, pl.ds(where_to, 8), :] = rotate_sums(group, lane_tile, sub_pair)
+        for p in range(2):
+            left = jnp.concatenate(
+                [
+                    tables[t][p * 16 : p * 16 + 16] * w[p * 16 : p * 16 + 16]
+                    for t in (1, 2)
+                    for w in weights
+                ],
+                axis=0,
+            )
+            right = jnp.concatenate(
+                [packed_ref[pl.ds(first + 96 * (2 * p + g) + 32, 64), :] for g in range(2)], axis=0
+            )
+            product = lax.dot_general(left, right, NT, preferred_element_type=jnp.float32)
+            for t in range(2):
+                group = []
+                for q in range(4):
+                    at = (t * 4 + q) * 16
+                    group.append(
+                        jnp.where(lane8 < 64, product[at : at + 8], product[at + 8 : at + 16])
+                    )
+                part_ref[1 + 2 * p + t, pl.ds(where_to, 8), :] = rotate_sums(
+                    group, lane_tile, sub_pair
+                )
+        return carry
+
+    lax.fori_loop(0, quads, one_quad, 0, unroll=UNROLL)
+
+    @pl.when(step == pl.num_programs(0) - 1)
+    def _():
+        sub = lax.broadcasted_iota(jnp.int32, (8, LANES), 0)
+        low = sub < 4
+        turn_sign = jnp.where(low, -1.0, 1.0)
+
+        def kind_tile(turned, at):
+            real = turned[at : at + 8] + turned[at + 8 : at + 16]
+            imag = turned[at + 16 : at + 24] + turned[at + 24 : at + 32]
+            real = real + pltpu.roll(real, 4, 0)
+            imag = imag + pltpu.roll(imag, 4, 0)
+            return jnp.where(low, real, imag)
+
+        for h in range(2):
+            for south in range(2):
+                for r in range(2):
+                    qr = (h * 2 + south) * 2 + r
+                    cycle = south * 2 + r
+                    row0 = cycle * 24 * 8 + h * 4
+                    turned = [
+                        part_ref[i, pl.ds(qr, all_quads_static(part_ref), stride=8), :].T
+                        for i in range(5)
+                    ]
+                    for g in range(4):
+                        at = 64 * (g % 2)
+                        plus = turned[1 + 2 * (g // 2)]
+                        minus = turned[2 + 2 * (g // 2)]
+                        temp = kind_tile(turned[0], g * 32)
+                        e_plus = kind_tile(plus, at)
+                        b_plus = kind_tile(plus, at + 32)
+                        e_minus = kind_tile(minus, at)
+                        b_minus = kind_tile(minus, at + 32)
+                        hemisphere = turn_sign * (-1.0 if south else 1.0)
+                        e_turn = pltpu.roll(e_minus, 4, 0) * hemisphere
+                        b_turn = pltpu.roll(b_minus, 4, 0) * hemisphere
+                        fields = (temp, -(e_plus + b_turn), e_turn - b_plus)
+                        for f in range(3):
+                            out_ref[pl.ds(row0 + f * 64 + g, 8, stride=8), :] = fields[f]
+
+
+def all_quads_static(part_ref):
+    return part_ref.shape[1] // 8
+
+
+UNROLL = 2
+
+
+def table_sums(legendre, harmonics, lower_here, first_column, full_width, interpret=False):
+    slots = harmonics.shape[0]
+    tables = (
+        legendre.reshape(3, slots, 2, 4, LANES).transpose(0, 1, 3, 2, 4).reshape(3, slots * 8, LANES)
+    )
+    packed = (
+        harmonics.reshape(slots, 3, 2, 4, 4, LANES)
+        .transpose(0, 1, 2, 4, 3, 5)
+        .reshape(slots * 96, LANES)
+    )
+    orders = jnp.broadcast_to(lower_here[:, None], (slots, LANES))
+    block = 32
+    return pl.pallas_call(
+        functools.partial(sums_kernel, full_width),
+        grid=(slots // block,),
+        in_specs=[
+            pl.BlockSpec(memory_space=pltpu.SMEM),
+            pl.BlockSpec((block, LANES), lambda i: (i, 0)),
+            pl.BlockSpec((3, block * 8, LANES), lambda i: (0, i, 0)),
+            pl.BlockSpec((block * 96, LANES), lambda i: (i, 0)),
+        ],
+        out_specs=pl.BlockSpec((768, LANES), lambda i: (0, 0)),
+        out_shape=jax.ShapeDtypeStruct((768, LANES), jnp.float32),
+        scratch_shapes=[
+            pltpu.VMEM((4, block * 8, LANES), jnp.bfloat16),
+            pltpu.VMEM((5, slots * 2, LANES), jnp.float32),
+        ],
+        compiler_params=pltpu.CompilerParams(
+            dimension_semantics=("arbitrary",), vmem_limit_bytes=64_000_000
+        ),
+        interpret=interpret,
+    )(first_column.reshape(1), orders, tables, packed)
+
+
+def synthesis_kernel(
+    sources, scalars_ref, orders_ref, sums_ref, phase_ref, first_ref, twist_ref, last_ref,
+    out_ref, left_ref, right_ref
+):
+    highest = lax.Precision.HIGHEST
+    owners = sums_ref.shape[0] // sources
+    tall = left_ref.shape[0] // 9
+    tall_ids = lax.broadcasted_iota(jnp.int32, (tall, LANES), 0)
+    lane_rows = lax.broadcasted_iota(jnp.int32, (LANES, LANES), 0)
+    for owner in range(owners):
+        total = sums_ref[owner * sources]
+        for source in range(1, sources):
+            total = total + sums_ref[owner * sources + source]
+        high = total.astype(jnp.bfloat16).astype(jnp.float32)
+        rest = total - high
+        middle = rest.astype(jnp.bfloat16).astype(jnp.float32)
+        pieces = (high, middle, rest - middle)
+        for k in range(8):
+            j = owner * 8 + k
+            order = orders_ref[j : j + 1, :]
+            right_ref[:, j * LANES : (j + 1) * LANES] = jnp.where(
+                lane_rows == order % LANES, 1.0, 0.0
+            ).astype(jnp.bfloat16)
+            here = tall_ids == order // LANES
+            for rr in range(3):
+                for i in range(3):
+                    at = (rr * 3 + i) * tall
+                    piece = pieces[i][rr * 8 + k : rr * 8 + k + 1, :]
+                    left_ref[at : at + tall, j * LANES : (j + 1) * LANES] = jnp.where(
+                        here, piece, 0.0
+                    ).astype(jnp.bfloat16)
+    placed = lax.dot_general(
+        left_ref[...], right_ref[...], NT, preferred_element_type=jnp.float32
+    )
+    shifted = scalars_ref[0] == 1
+    factor = phase_ref[2]
+    cosine = jnp.where(shifted, phase_ref[0], factor)
+    sine = jnp.where(shifted, phase_ref[1], 0.0)
+    half = 2 * tall
+    for rr in range(3):
+        at = rr * 3 * tall
+        value = (
+            placed[at : at + tall]
+            + placed[at + tall : at + 2 * tall]
+            + placed[at + 2 * tall : at + 3 * tall]
+        )
+        is_real = scalars_ref[1 + rr] == 0
+        spectrum = jnp.concatenate(
+            [
+                value * jnp.where(is_real, cosine, -sine),
+                value * jnp.where(is_real, sine, cosine),
+            ],
+            axis=0,
+        )
+        first = jnp.dot(
+            first_ref[...], spectrum, precision=highest, preferred_element_type=jnp.float32
+        )
+        real, imag = first[:half], first[half:]
+        twisted = jnp.concatenate(
+            [
+                real * twist_ref[0] - imag * twist_ref[1],
+                real * twist_ref[1] + imag * twist_ref[0],
+            ],
+            axis=1,
+        )
+        both = lax.dot_general(
+            last_ref[...], twisted, NT, precision=highest, preferred_element_type=jnp.float32
+        )
+        pixels = jnp.concatenate([both[:64], both[64:]], axis=1)
+        for e in range(out_ref.shape[0]):
+            out_ref[e, rr * 8 : rr * 8 + 8, :] = pixels[e * 8 : e * 8 + 8]
+
+
+def synthesis_tables(orders_count):
+    pixels = 2 * orders_count
+    tall = orders_count // LANES
+    half = 2 * tall
+    orders = np.arange(orders_count).reshape(tall, LANES)
+    factor = np.where(orders == 0, 1.0, 2.0)
+    angle = orders * (np.pi / pixels)
+    phase = np.stack([np.cos(angle) * factor, np.sin(angle) * factor, factor])
+    angle = (np.arange(half)[:, None] * np.arange(tall)[None, :] % half) * (2 * np.pi / half)
+    first = np.block([[np.cos(angle), -np.sin(angle)], [np.sin(angle), np.cos(angle)]])
+    angle = np.arange(half)[:, None] * np.arange(LANES)[None, :] * (2 * np.pi / pixels)
+    twist = np.stack([np.cos(angle), np.sin(angle)])
+    ids = np.concatenate([np.arange(0, LANES, 2), np.arange(1, LANES, 2)])
+    angle = (ids[:, None] * np.arange(LANES)[None, :] % LANES) * (2 * np.pi / LANES)
+    last = np.concatenate([np.cos(angle), -np.sin(angle)], axis=1)
+    return [jnp.asarray(t, jnp.float32) for t in (phase, first, twist, last)]
+
+
+def synthesis(received, orders, scalars, sources, orders_count, interpret=False):
+    tall = orders_count // LANES
+    vmem = pl.BlockSpec(memory_space=pltpu.VMEM)
+    return pl.pallas_call(
+        functools.partial(synthesis_kernel, sources),
+        in_specs=[pl.BlockSpec(memory_space=pltpu.SMEM)] + [vmem] * 6,
+        out_specs=vmem,
+        out_shape=jax.ShapeDtypeStruct((sources, 24, LANES), jnp.float32),
+        scratch_shapes=[
+            pltpu.VMEM((9 * tall, orders_count), jnp.bfloat16),
+            pltpu.VMEM((LANES, orders_count), jnp.bfloat16),
+        ],
+        compiler_params=pltpu.CompilerParams(vmem_limit_bytes=32 * 1024 * 1024),
+        interpret=interpret,
+    )(scalars, orders, received, *synthesis_tables(orders_count))
+
+
+def slot_layout(slot_orders, owners):
+    full_width = 2 * slot_orders.shape[0]
+    lower = slot_orders.reshape(owners, LANES, 4).transpose(0, 2, 1)
+    return jnp.stack([lower, full_width - 1 - lower], axis=1).reshape(owners * 8, LANES)
+
+
+def packed_body(legendre, harmonics, slot_orders, cycle_index):
+    owners = lax.axis_size("ma")
+    sources = lax.axis_size("ell")
+    slots_here = harmonics.shape[0]
+    columns_here = harmonics.shape[-1]
+    full_width = 2 * slot_orders.shape[0]
+    pairs = cycle_index.shape[0]
+    me, part = lax.axis_index("ma"), lax.axis_index("ell")
+    lower_here = lax.dynamic_slice_in_dim(slot_orders, me * slots_here, slots_here)
+    sums = table_sums(legendre, harmonics, lower_here, part * columns_here, full_width)
+    received = lax.all_to_all(
+        sums.reshape(owners * sources, 24, LANES), ("ma", "ell"), 0, 0, tiled=True
+    )
+    shift = cycle_index[me % pairs] % 2
+    row = part * 3 + jnp.arange(3, dtype=jnp.int32)
+    scalars = jnp.concatenate([shift[None], (row // 4) % 2])
+    maps = synthesis(received, slot_layout(slot_orders, owners), scalars, sources, full_width)
+    pixels = lax.all_to_all(maps, "ell", 0, 0, tiled=True)
+    fields = pixels.reshape(3, 2, 4, 8, LANES)
+    return (fields[:, 0] + fields[:, 1]).reshape(1, 3, 4, 8 * LANES)
+
+
+def body(legendre, harmonics, slot_orders, cycle_index):
+    owners, sources = lax.axis_size("ma"), lax.axis_size("ell")
+    slots, kinds, parts, components, columns = harmonics.shape
+    pairs = cycle_index.shape[0]
+    fits = (
+        (pairs, components, columns, slots) == (2, 4, 4 * LANES, 4 * LANES)
+        and owners == 2 * pairs
+        and kinds * parts * components == 3 * sources
+        and slot_orders.shape[0] * 4 == sources * 8 * LANES
+    )
+    chosen = packed_body if fits else general_body
+    return chosen(legendre, harmonics, slot_orders, cycle_index)
+
+
 def solution(mesh):
     return jax.shard_map(
         body,

time: 595 us -> 61.4 us (0.10)
  matrix products: 392 us -> 0 us
  other arithmetic: 59.1 us -> 0.14 us
  waiting for transfers between devices: 67.2 us -> 10.2 us
  local copies, waits for them, and re-layouts: 51.4 us -> 3.39 us
  Pallas kernels: 0 us -> 27.8 us
  between operations: 16.2 us -> 2.06 us
  blocking collectives: 0 us -> 10.1 us
    dot_general x13 -> x0, matrix products: 392 us -> none  [the longest x1 152 us: body(): jnp.einsum('srj,sqkpcj->srqkpc', legendre[2], packed[:, :, 1:3], preferre...]
    psum x1 -> x0, waiting for transfers between devices: 60 us -> none  [body(): summed = lax.psum(cycle_sums, 'ell')]
    mul x3 -> x0, other arithmetic: 41.7 us -> none  [the longest x1 41.5 us: body(): packed = harmonics[:, None] * weights[:, :, None, None, None, :]]
    pallas_call x0 -> x2, Pallas kernels: none -> 27.8 us  [the longest x1 24.4 us: table_sums(): pl.pallas_call(functools.partial(sums_kernel, full_width), grid=(slots //...]
    another operation x7 -> x2, other arithmetic: 16.1 us -> 0.03 us  [slot_layout(): jnp.stack([lower, full_width - 1 - lower], axis=1)]
    unnamed x12, local copies, waits for them, and re-layouts: 14.2 us -> 0.02 us
    gather x2 -> x0, local copies, waits for them, and re-layouts: 12.4 us -> none  [the longest x1 11.8 us: body(): lower_all = slot_orders[slot_ids]]
    reshape x3 -> x1, local copies, waits for them, and re-layouts: 11.4 us -> 0.25 us  [slot_layout(): lower = slot_orders.reshape(owners, LANES, 4).transpose(0, 2, 1)]
  transfers between devices with their start and end apart: 2 -> 1, of which waited for: 2 -> 1; matrix products, arithmetic and copies ran while one was open for 2% -> 2% of each run, Pallas kernels for 0% -> 0%
where the time goes in v1:
time: 61.4 us; the launch traced here: 61 us
  Pallas kernels  27.8 us (45%)
  waiting for transfers between devices  10.2 us (17%)
  blocking collectives  10.1 us (16%)
  starting transfers between devices  7.37 us (12%)
  local copies, waits for them, and re-layouts  3.39 us (6%)
  between operations  2.06 us (3%)
    pallas_call x1, Pallas kernels, table_sums(): pl.pallas_call(functools.partial(sums_kernel, full_width), grid=(slots //...  24.4 us
    all_to_all x1, waiting for transfers between devices, packed_body(): lax.all_to_all(sums.reshape(owners * sources, 24, LANES), ('ma', 'ell'),...  10.2 us
    all_to_all x1, blocking collectives, packed_body(): pixels = lax.all_to_all(maps, 'ell', 0, 0, tiled=True)  10.1 us
    all_to_all x1, starting transfers between devices, packed_body(): lax.all_to_all(sums.reshape(owners * sources, 24, LANES), ('ma', 'ell'),...  7.37 us
    pallas_call x1, Pallas kernels, synthesis(): pl.pallas_call(functools.partial(synthesis_kernel, sources), in_specs=[pl...  3.37 us
  transfers between devices with their start and end apart: 1, of which 1 were waited for; matrix products, arithmetic and copies ran while one was open for 2% of the time, Pallas kernels for 0%

profile of v1, /device:TPU:0, one launch (start us, length us, event | category | flops | bytes accessed | tf_op | source)
XLA Modules:
  0.0 61.0 jit_solution(17680321487849814560)
XLA Ops:
  0.0 0.0 copy-start
  0.0 0.0 copy-start.1
  0.0 0.0 copy-start.2
  0.0 0.0 copy-start.3
  0.0 0.0 copy-start.5
  0.0 0.8 %dynamic_slice.7 = s32[512]{0:T(512)S(1)} dynamic-slice(s32[2048]{0:T(1024)} %param.10, s32[]{:T(128)S(6)} %select_n.33), dynamic_slice_sizes={512} | dynamic-slice | bytes 4100 | tf_op jit(solution)/shard_map/dynamic_slice | solution.py:457
  0.9 0.8 %broadcast_in_dim.10.orders_ref = s32[512,128]{1,0:T(8,128)} broadcast(s32[512]{0:T(512)S(1)} %dynamic_slice.7), dimensions={0} | broadcast | bytes 264192 | tf_op jit(solution)/shard_map/broadcast_in_dim | solution.py:311
  1.7 24.4 %shard_map.82 = f32[768,128]{1,0:T(8,128)} custom-call(s32[1]{0:T(128)} %bitcast.6.start_ref, s32[512,128]{1,0:T(8,128)} %broadcast_in_dim.10.orders_ref, bf16[3,4096,128]{2,1,0:T(8,128)(2,1)} %bitcast.28, bf16[49152,128]{1,0:T(8,128)(2,1)} %bitcast.27), custom_call_target="tpu_custom_call" | custom-call | tf_op jit(solution)/shard_map/pallas_call | solution.py:313
  26.1 7.4 %all-to-all-start = ((f32[32,24,128]{2,1,0:T(8,128)}), f32[32,24,128]{2,1,0:T(8,128)S(1)}, u32[]{:S(2)}, u32[]{:S(2)}) async-start(f32[32,24,128]{2,1,0:T(8,128)} %bitcast.30), calls=%async_computation | async-start | bytes 786432 | tf_op jit(solution)/shard_map/all_to_all | solution.py:459
  33.5 0.0 copy-done.5
  33.5 0.6 dynamic_slice.6
  36.0 0.0 copy-done.4
  36.1 0.3 reshape.47
  36.3 0.1 copy.15
  36.5 0.1 copy.16
  36.6 0.1 pad_add_fusion.1.scalars_ref
  36.7 10.2 %all-to-all-done.sums_ref = f32[32,24,128]{2,1,0:T(8,128)S(1)} async-done(((f32[32,24,128]{2,1,0:T(8,128)}), f32[32,24,128]{2,1,0:T(8,128)S(1)}, u32[]{:S(2)}, u32[]{:S(2)}) %all-to-all-start) | async-done | bytes 393248 | tf_op jit(solution)/shard_map/all_to_all | solution.py:459
  46.9 0.0 copy-done
  46.9 0.0 copy-done.1
  46.9 0.0 copy-done.2
  46.9 0.0 copy-done.3
  46.9 3.4 %shard_map.83 = f32[8,24,128]{2,1,0:T(8,128)S(1)} custom-call(s32[4]{0:T(128)S(1)} %pad_add_fusion.1.scalars_ref, s32[32,128]{1,0:T(8,128)S(1)} %bitcast.26, f32[32,24,128]{2,1,0:T(8,128)S(1)} %all-to-all-done.sums_ref, f32[3,32,128]{2,1,0:T(8,128)S(1)} %copy-done.3, f32[128,64]{1,0:T(8,128)S(1)} %copy-done.2, f32[2,64,128]{2,1,0:T(8,128)S(1)} %copy-done.1, ...), custom_call_target="tpu_custom_call" | custom-call | tf_op jit(solution)/shard_map/pallas_call | solution.py:429
  50.3 10.1 %all_to_all.10 = f32[8,24,128]{2,1,0:T(8,128)S(1)} all-to-all(f32[8,24,128]{2,1,0:T(8,128)S(1)} %shard_map.83), channel_id=1, replica_groups=mesh['ma'=4,'ell'=8] {'ell'}, dimensions={0} | all-to-all | bytes 196608 | tf_op jit(solution)/shard_map/all_to_all | solution.py:466
  60.4 0.6 %add.47 = f32[1,3,4,1024]{3,2,1,0:T(4,128)} reshape(f32[3,1,4,8,128]{4,3,2,1,0:T(8,128)S(1)} %slice_add_fusion) | data formatting | bytes 98304 | tf_op jit(solution)/shard_map/add | solution.py:468
  (5 shorter events, 0.1 us)
Async XLA Ops:
  0.0 46.9 %copy-start = (f32[128,256]{1,0:T(8,128)S(1)}, f32[128,256]{1,0:T(8,128)}, u32[]{:S(2)}) copy-start(f32[128,256]{1,0:T(8,128)} %constant.65.clone.last_ref) | copy-start | bytes 393220
  0.0 46.9 %copy-start.1 = (f32[2,64,128]{2,1,0:T(8,128)S(1)}, f32[2,64,128]{2,1,0:T(8,128)}, u32[]{:S(2)}) copy-start(f32[2,64,128]{2,1,0:T(8,128)} %constant.64.clone.twist_ref) | copy-start | bytes 196612
  0.0 46.9 %copy-start.2 = (f32[128,64]{1,0:T(8,128)S(1)}, f32[128,64]{1,0:T(8,128)}, u32[]{:S(2)}) copy-start(f32[128,64]{1,0:T(8,128)} %constant.63.clone.first_ref) | copy-start | bytes 98308
  0.0 46.9 %copy-start.3 = (f32[3,32,128]{2,1,0:T(8,128)S(1)}, f32[3,32,128]{2,1,0:T(8,128)}, u32[]{:S(2)}) copy-start(f32[3,32,128]{2,1,0:T(8,128)} %constant.62.clone.phase_ref) | copy-start | bytes 147460
  0.0 36.0 %copy-start.4 = (s32[2048]{0:T(1024)S(1)}, s32[2048]{0:T(1024)}, u32[]{:S(2)}) copy-start(s32[2048]{0:T(1024)} %param.10) | copy-start | bytes 24580
  0.0 33.5 %copy-start.5 = (s32[2]{0:T(128)S(1)}, s32[2]{0:T(128)}, u32[]{:S(2)}) copy-start(s32[2]{0:T(128)} %param.11) | copy-start | bytes 28
  26.1 20.8 %all-to-all-start = ((f32[32,24,128]{2,1,0:T(8,128)}), f32[32,24,128]{2,1,0:T(8,128)S(1)}, u32[]{:S(2)}, u32[]{:S(2)}) async-start(f32[32,24,128]{2,1,0:T(8,128)} %bitcast.30), calls=%async_computation | async-start | bytes 786432 | tf_op jit(solution)/shard_map/all_to_all | solution.py:459

commit v2 on v1

--- a/solution.py
+++ b/solution.py
@@ -179,34 +179,33 @@
     return turned
 
 
-def sums_kernel(full_width, start_ref, orders_ref, table_ref, packed_ref, out_ref, weight_ref, part_ref):
+def sums_kernel(full_width, columns, slots, orders_ref, table_ref, packed_ref, out_ref, part_ref):
     step = pl.program_id(0)
-    slots = orders_ref.shape[0]
-    quads = slots // 4
-    all_quads = pl.num_programs(0) * quads
-    rows = slots * 8
-    lower = jnp.broadcast_to(orders_ref[...][:, None, :], (slots, 8, LANES)).reshape(rows, LANES)
-    row = lax.broadcasted_iota(jnp.int32, (rows, LANES), 0)
-    lane = lax.broadcasted_iota(jnp.int32, (rows, LANES), 1)
-    column = start_ref[0] + ((row % 8) // 2) * LANES + lane
-    is_lower = column < full_width - 1 - lower
-    is_upper = jnp.logical_and(jnp.logical_not(is_lower), column < full_width - 1)
-    lower_sign = (1 - 2 * (column % 2)).astype(jnp.float32)
-    upper_sign = (1 - 2 * ((column + 1 + lower) % 2)).astype(jnp.float32)
-    lower_part = jnp.where(is_lower, 1.0, 0.0)
-    upper_part = jnp.where(is_upper, 1.0, 0.0)
-    weight_ref[0] = lower_part.astype(jnp.bfloat16)
-    weight_ref[1] = (lower_part * lower_sign).astype(jnp.bfloat16)
-    weight_ref[2] = upper_part.astype(jnp.bfloat16)
-    weight_ref[3] = (upper_part * upper_sign).astype(jnp.bfloat16)
-
+    block = table_ref.shape[1] // 8
+    quads = block // 4
+    first_slot = lax.axis_index("ma") * slots + step * block
+    first_column = lax.axis_index("ell") * columns
     sub_pair = lax.broadcasted_iota(jnp.int32, (8, LANES), 0) // 2
     lane8 = lax.broadcasted_iota(jnp.int32, (8, LANES), 1)
     lane_tile = (lane8 % 16) // 4
 
+    column = first_column + sub_pair * LANES + lane8
+    alternate = (1 - 2 * (column % 2)).astype(jnp.float32)
+    inside = column < full_width - 1
+
     def one_quad(quad, carry):
         base = pl.multiple_of(quad * 32, 32)
-        weights = [weight_ref[q, pl.ds(base, 32), :] for q in range(4)]
+        parts = [[], [], [], []]
+        for g in range(4):
+            lower = orders_ref[first_slot + quad * 4 + g]
+            is_lower = column < full_width - 1 - lower
+            is_upper = jnp.logical_and(jnp.logical_not(is_lower), inside)
+            upper_sign = alternate * (2 * (lower % 2) - 1).astype(jnp.float32)
+            parts[0].append(jnp.where(is_lower, 1.0, 0.0))
+            parts[1].append(jnp.where(is_lower, alternate, 0.0))
+            parts[2].append(jnp.where(is_upper, 1.0, 0.0))
+            parts[3].append(jnp.where(is_upper, upper_sign, 0.0))
+        weights = [jnp.concatenate(p, axis=0).astype(jnp.bfloat16) for p in parts]
         tables = [table_ref[t, pl.ds(base, 32), :] for t in range(3)]
         first = pl.multiple_of(quad * 384, 32)
         where_to = pl.multiple_of((step * quads + quad) * 8, 8)
@@ -298,8 +297,9 @@
 UNROLL = 2
 
 
-def table_sums(legendre, harmonics, lower_here, first_column, full_width, interpret=False):
-    slots = harmonics.shape[0]
+def table_sums(legendre, harmonics, slot_orders):
+    slots, columns = harmonics.shape[0], harmonics.shape[-1]
+    full_width = 2 * slot_orders.shape[0]
     tables = (
         legendre.reshape(3, slots, 2, 4, LANES).transpose(0, 1, 3, 2, 4).reshape(3, slots * 8, LANES)
     )
@@ -308,54 +308,101 @@
         .transpose(0, 1, 2, 4, 3, 5)
         .reshape(slots * 96, LANES)
     )
-    orders = jnp.broadcast_to(lower_here[:, None], (slots, LANES))
     block = 32
     return pl.pallas_call(
-        functools.partial(sums_kernel, full_width),
+        functools.partial(sums_kernel, full_width, columns, slots),
         grid=(slots // block,),
         in_specs=[
             pl.BlockSpec(memory_space=pltpu.SMEM),
-            pl.BlockSpec((block, LANES), lambda i: (i, 0)),
             pl.BlockSpec((3, block * 8, LANES), lambda i: (0, i, 0)),
             pl.BlockSpec((block * 96, LANES), lambda i: (i, 0)),
         ],
         out_specs=pl.BlockSpec((768, LANES), lambda i: (0, 0)),
         out_shape=jax.ShapeDtypeStruct((768, LANES), jnp.float32),
         scratch_shapes=[
-            pltpu.VMEM((4, block * 8, LANES), jnp.bfloat16),
             pltpu.VMEM((5, slots * 2, LANES), jnp.float32),
         ],
         compiler_params=pltpu.CompilerParams(
             dimension_semantics=("arbitrary",), vmem_limit_bytes=64_000_000
         ),
-        interpret=interpret,
-    )(first_column.reshape(1), orders, tables, packed)
+    )(slot_orders, tables, packed)
 
 
 def synthesis_kernel(
-    sources, scalars_ref, orders_ref, sums_ref, phase_ref, first_ref, twist_ref, last_ref,
-    out_ref, left_ref, right_ref
+    scalars_ref, orders_ref, sums_ref, phase_ref, first_ref, twist_ref, last_ref, out_ref,
+    left_ref, right_ref, held_ref, pixel_ref, landed_ref, send_sem, recv_sem, pixel_send, pixel_recv
 ):
     highest = lax.Precision.HIGHEST
-    owners = sums_ref.shape[0] // sources
+    owners, sources = lax.axis_size("ma"), lax.axis_size("ell")
+    my_owner, my_source = lax.axis_index("ma"), lax.axis_index("ell")
+    me = my_owner * sources + my_source
+    mesh_ids = pl.DeviceIdType.MESH
+    count = owners * sources
+
+    def shifted_device(step):
+        owner = lax.rem(my_owner + step // sources, owners)
+        source = lax.rem(my_source + step % sources, sources)
+        return owner, source
+
+    barrier = pltpu.get_barrier_semaphore()
+
+    def greet(step, carry):
+        pl.semaphore_signal(
+            barrier, inc=1, device_id=shifted_device(step), device_id_type=mesh_ids
+        )
+        return carry
+
+    lax.fori_loop(1, count, greet, 0)
+    pl.semaphore_wait(barrier, count - 1)
+
+    def exchange(step):
+        owner, source = shifted_device(step)
+        return pltpu.make_async_remote_copy(
+            src_ref=sums_ref.at[owner * sources + source],
+            dst_ref=held_ref.at[me],
+            send_sem=send_sem.at[step],
+            recv_sem=recv_sem.at[step],
+            device_id=(owner, source),
+            device_id_type=mesh_ids,
+        )
+
+    def send(step, carry):
+        exchange(step).start()
+        return carry
+
+    lax.fori_loop(1, count, send, 0)
+    held_ref[me] = sums_ref[me]
+
     tall = left_ref.shape[0] // 9
     tall_ids = lax.broadcasted_iota(jnp.int32, (tall, LANES), 0)
     lane_rows = lax.broadcasted_iota(jnp.int32, (LANES, LANES), 0)
-    for owner in range(owners):
-        total = sums_ref[owner * sources]
+
+    def await_step(step, carry):
+        exchange(step).wait()
+        return carry
+
+    for near in range(owners):
+        owner = lax.rem(my_owner + owners - near, owners)
+        ordered = orders_ref[pl.ds(pl.multiple_of(owner * 8, 8), 8), :]
+        for k in range(8):
+            j = near * 8 + k
+            right_ref[:, j * LANES : (j + 1) * LANES] = jnp.where(
+                lane_rows == ordered[k : k + 1, :] % LANES, 1.0, 0.0
+            ).astype(jnp.bfloat16)
+    for near in range(owners):
+        owner = lax.rem(my_owner + owners - near, owners)
+        ordered = orders_ref[pl.ds(pl.multiple_of(owner * 8, 8), 8), :]
+        lax.fori_loop(max(1, near * sources), (near + 1) * sources, await_step, 0)
+        total = held_ref[owner * sources]
         for source in range(1, sources):
-            total = total + sums_ref[owner * sources + source]
+            total = total + held_ref[owner * sources + source]
         high = total.astype(jnp.bfloat16).astype(jnp.float32)
         rest = total - high
         middle = rest.astype(jnp.bfloat16).astype(jnp.float32)
         pieces = (high, middle, rest - middle)
         for k in range(8):
-            j = owner * 8 + k
-            order = orders_ref[j : j + 1, :]
-            right_ref[:, j * LANES : (j + 1) * LANES] = jnp.where(
-                lane_rows == order % LANES, 1.0, 0.0
-            ).astype(jnp.bfloat16)
-            here = tall_ids == order // LANES
+            j = near * 8 + k
+            here = tall_ids == ordered[k : k + 1, :] // LANES
             for rr in range(3):
                 for i in range(3):
                     at = (rr * 3 + i) * tall
@@ -371,6 +418,19 @@
     cosine = jnp.where(shifted, phase_ref[0], factor)
     sine = jnp.where(shifted, phase_ref[1], 0.0)
     half = 2 * tall
+
+    def pixel_copy(rr, step):
+        source = lax.rem(my_source + step, sources)
+        rows = pl.ds(rr * 8, 8)
+        return pltpu.make_async_remote_copy(
+            src_ref=pixel_ref.at[source, rows],
+            dst_ref=landed_ref.at[my_source, rows],
+            send_sem=pixel_send.at[rr, step],
+            recv_sem=pixel_recv.at[rr, step],
+            device_id=(my_owner, source),
+            device_id_type=mesh_ids,
+        )
+
     for rr in range(3):
         at = rr * 3 * tall
         value = (
@@ -400,9 +460,29 @@
         both = lax.dot_general(
             last_ref[...], twisted, NT, precision=highest, preferred_element_type=jnp.float32
         )
-        pixels = jnp.concatenate([both[:64], both[64:]], axis=1)
-        for e in range(out_ref.shape[0]):
-            out_ref[e, rr * 8 : rr * 8 + 8, :] = pixels[e * 8 : e * 8 + 8]
+        pixels = jnp.concatenate([both[:half], both[half:]], axis=1)
+        for e in range(sources):
+            pixel_ref[e, rr * 8 : rr * 8 + 8, :] = pixels[e * 8 : e * 8 + 8]
+        if rr > 0:
+            for step in range(1, sources):
+                pixel_copy(rr - 1, step).start()
+    landed_ref[my_source] = pixel_ref[my_source]
+    for step in range(1, sources):
+        pixel_copy(0, step).wait_send()
+    for step in range(1, sources):
+        pixel_copy(2, step).start()
+    for step in range(1, sources):
+        pixel_copy(0, step).wait_recv()
+        pixel_copy(1, step).wait()
+    for step in range(1, sources):
+        pixel_copy(2, step).wait()
+    for f in range(3):
+        for c in range(4):
+            real, imag = f * 8 + c, f * 8 + 4 + c
+            out_ref[f * 4 + c] = (
+                landed_ref[real // 3, real % 3 * 8 : real % 3 * 8 + 8]
+                + landed_ref[imag // 3, imag % 3 * 8 : imag % 3 * 8 + 8]
+            )
 
 
 def synthesis_tables(orders_count):
@@ -423,21 +503,30 @@
     return [jnp.asarray(t, jnp.float32) for t in (phase, first, twist, last)]
 
 
-def synthesis(received, orders, scalars, sources, orders_count, interpret=False):
+def synthesis(sums, orders, scalars, sources, orders_count):
     tall = orders_count // LANES
     vmem = pl.BlockSpec(memory_space=pltpu.VMEM)
+    pixels = (sources, 24, LANES)
     return pl.pallas_call(
-        functools.partial(synthesis_kernel, sources),
+        synthesis_kernel,
         in_specs=[pl.BlockSpec(memory_space=pltpu.SMEM)] + [vmem] * 6,
         out_specs=vmem,
-        out_shape=jax.ShapeDtypeStruct((sources, 24, LANES), jnp.float32),
+        out_shape=jax.ShapeDtypeStruct((12, 8, LANES), jnp.float32),
         scratch_shapes=[
             pltpu.VMEM((9 * tall, orders_count), jnp.bfloat16),
             pltpu.VMEM((LANES, orders_count), jnp.bfloat16),
+            pltpu.VMEM(sums.shape, jnp.float32),
+            pltpu.VMEM(pixels, jnp.float32),
+            pltpu.VMEM(pixels, jnp.float32),
+            pltpu.SemaphoreType.DMA((sums.shape[0],)),
+            pltpu.SemaphoreType.DMA((sums.shape[0],)),
+            pltpu.SemaphoreType.DMA((3, sources)),
+            pltpu.SemaphoreType.DMA((3, sources)),
         ],
-        compiler_params=pltpu.CompilerParams(vmem_limit_bytes=32 * 1024 * 1024),
-        interpret=interpret,
-    )(scalars, orders, received, *synthesis_tables(orders_count))
+        compiler_params=pltpu.CompilerParams(
+            vmem_limit_bytes=32 * 1024 * 1024, collective_id=0, has_side_effects=True
+        ),
+    )(scalars, orders, sums, *synthesis_tables(orders_count))
 
 
 def slot_layout(slot_orders, owners):
@@ -449,23 +538,21 @@
 def packed_body(legendre, harmonics, slot_orders, cycle_index):
     owners = lax.axis_size("ma")
     sources = lax.axis_size("ell")
-    slots_here = harmonics.shape[0]
-    columns_here = harmonics.shape[-1]
     full_width = 2 * slot_orders.shape[0]
     pairs = cycle_index.shape[0]
     me, part = lax.axis_index("ma"), lax.axis_index("ell")
-    lower_here = lax.dynamic_slice_in_dim(slot_orders, me * slots_here, slots_here)
-    sums = table_sums(legendre, harmonics, lower_here, part * columns_here, full_width)
-    received = lax.all_to_all(
-        sums.reshape(owners * sources, 24, LANES), ("ma", "ell"), 0, 0, tiled=True
-    )
     shift = cycle_index[me % pairs] % 2
     row = part * 3 + jnp.arange(3, dtype=jnp.int32)
     scalars = jnp.concatenate([shift[None], (row // 4) % 2])
-    maps = synthesis(received, slot_layout(slot_orders, owners), scalars, sources, full_width)
-    pixels = lax.all_to_all(maps, "ell", 0, 0, tiled=True)
-    fields = pixels.reshape(3, 2, 4, 8, LANES)
-    return (fields[:, 0] + fields[:, 1]).reshape(1, 3, 4, 8 * LANES)
+    sums = table_sums(legendre, harmonics, slot_orders)
+    maps = synthesis(
+        sums.reshape(owners * sources, 24, LANES),
+        slot_layout(slot_orders, owners),
+        scalars,
+        sources,
+        full_width,
+    )
+    return maps.reshape(1, 3, 4, 8 * LANES)
 
 
 def body(legendre, harmonics, slot_orders, cycle_index):

time: 61.4 us -> 55.9 us (0.910)
  Pallas kernels: 27.8 us -> 49.1 us
  waiting for transfers between devices: 10.2 us -> 0 us
  blocking collectives: 10.1 us -> 0 us
  starting transfers between devices: 7.37 us -> 0 us
  local copies, waits for them, and re-layouts: 3.39 us -> 4.09 us
    pallas_call x2, Pallas kernels: 27.8 us -> 49.1 us  [the longest x1 27.5 us: synthesis(): pl.pallas_call(synthesis_kernel, in_specs=[pl.BlockSpec(memory_space=pltp...]
    all_to_all x1 -> x0, waiting for transfers between devices: 10.2 us -> none  [packed_body(): lax.all_to_all(sums.reshape(owners * sources, 24, LANES), ('ma', 'ell'),...]
    all_to_all x1 -> x0, blocking collectives: 10.1 us -> none  [packed_body(): pixels = lax.all_to_all(maps, 'ell', 0, 0, tiled=True)]
    all_to_all x1 -> x0, starting transfers between devices: 7.37 us -> none  [packed_body(): lax.all_to_all(sums.reshape(owners * sources, 24, LANES), ('ma', 'ell'),...]
    unnamed x12 -> x10, local copies, waits for them, and re-layouts: 0.02 us -> 1 us
    broadcast_in_dim x1 -> x0, local copies, waits for them, and re-layouts: 0.84 us -> none  [table_sums(): orders = jnp.broadcast_to(lower_here[:, None], (slots, LANES))]
    dynamic_slice x1 -> x0, local copies, waits for them, and re-layouts: 0.84 us -> none  [packed_body(): lax.dynamic_slice_in_dim(slot_orders, me * slots_here, slots_here)]
    dynamic_slice x1, local copies, waits for them, and re-layouts: 0.59 us -> 1.29 us  [packed_body(): shift = cycle_index[me % pairs] % 2]
  transfers between devices with their start and end apart: 1 -> 0, of which waited for: 1 -> 0; matrix products, arithmetic and copies ran while one was open for 2% -> 0% of each run, Pallas kernels for 0% -> 0%
where the time goes in v2:
time: 55.9 us; the launch traced here: 55.3 us
  Pallas kernels  49.1 us (88%)
  local copies, waits for them, and re-layouts  4.09 us (7%)
  between operations  2.01 us (4%)
    pallas_call x1, Pallas kernels, synthesis(): pl.pallas_call(synthesis_kernel, in_specs=[pl.BlockSpec(memory_space=pltp...  27.5 us
    pallas_call x1, Pallas kernels, table_sums(): pl.pallas_call(functools.partial(sums_kernel, full_width, columns, slots)...  21.6 us
    dynamic_slice x1, local copies, waits for them, and re-layouts, packed_body(): shift = cycle_index[me % pairs] % 2  1.29 us

profile of v2, /device:TPU:0, one launch (start us, length us, event | category | flops | bytes accessed | tf_op | source)
XLA Modules:
  0.0 55.3 jit_solution(13977196616474921913)
XLA Ops:
  0.0 0.0 copy-start.1
  0.0 0.0 copy-start.2
  0.0 0.0 copy-start.3
  0.0 0.0 copy-start.4
  0.0 1.3 %dynamic_slice.3 = s32[1]{0:T(128)} dynamic-slice(s32[2]{0:T(128)} %param.11, s32[]{:T(128)S(6)} %select_n.26), dynamic_slice_sizes={1} | dynamic-slice | bytes 12 | tf_op jit(solution)/shard_map/dynamic_slice | solution.py:544
  3.3 0.1 pad_add_fusion.1.scalars_ref
  3.3 0.9 %reshape.24 = s32[4,128,4]{2,1,0:T(8,128)S(1)} reshape(s32[2048]{0:T(1024)} %orders_ref.1) | data formatting | bytes 16384 | tf_op jit(solution)/shard_map/reshape | solution.py:534
  4.3 0.1 copy.15
  4.4 0.1 copy.16
  4.6 21.6 %shard_map.82 = f32[768,128]{1,0:T(8,128)} custom-call(s32[2048]{0:T(1024)} %orders_ref.1, bf16[3,4096,128]{2,1,0:T(8,128)(2,1)} %bitcast.25, bf16[49152,128]{1,0:T(8,128)(2,1)} %bitcast.24), custom_call_target="tpu_custom_call" | custom-call | tf_op jit(solution)/shard_map/pallas_call | solution.py:312
  26.2 0.0 copy-done.1
  26.2 0.0 copy-done.2
  26.2 0.0 copy-done.3
  26.2 0.0 copy-done.4
  26.2 0.0 copy-start
  26.2 1.0 %copy-done = f32[768,128]{1,0:T(8,128)S(1)} copy-done((f32[768,128]{1,0:T(8,128)S(1)}, f32[768,128]{1,0:T(8,128)}, u32[]{:S(2)}) %copy-start) | copy-done | bytes 393240
  27.2 27.5 %shard_map.83 = f32[12,8,128]{2,1,0:T(8,128)S(1)} custom-call(s32[4]{0:T(128)S(1)} %pad_add_fusion.1.scalars_ref, s32[32,128]{1,0:T(8,128)S(1)} %bitcast.23, f32[32,24,128]{2,1,0:T(8,128)S(1)} %bitcast.22, f32[3,32,128]{2,1,0:T(8,128)S(1)} %copy-done.4, f32[128,64]{1,0:T(8,128)S(1)} %copy-done.3, f32[2,64,128]{2,1,0:T(8,128)S(1)} %copy-done.2, ...), custom_call_target="tpu_custom_call" | custom-call | tf_op jit(solution)/shard_map/pallas_call | solution.py:510
  54.7 0.6 %reshape.31 = f32[1,3,4,1024]{3,2,1,0:T(4,128)} reshape(f32[12,8,128]{2,1,0:T(8,128)S(1)} %shard_map.83) | data formatting | bytes 98304 | tf_op jit(solution)/shard_map/reshape | solution.py:555
  (3 shorter events, 0.1 us)
Async XLA Ops:
  0.0 26.2 %copy-start.1 = (f32[128,256]{1,0:T(8,128)S(1)}, f32[128,256]{1,0:T(8,128)}, u32[]{:S(2)}) copy-start(f32[128,256]{1,0:T(8,128)} %constant.61.clone.last_ref) | copy-start | bytes 393220
  0.0 26.2 %copy-start.2 = (f32[2,64,128]{2,1,0:T(8,128)S(1)}, f32[2,64,128]{2,1,0:T(8,128)}, u32[]{:S(2)}) copy-start(f32[2,64,128]{2,1,0:T(8,128)} %constant.60.clone.twist_ref) | copy-start | bytes 196612
  0.0 26.2 %copy-start.3 = (f32[128,64]{1,0:T(8,128)S(1)}, f32[128,64]{1,0:T(8,128)}, u32[]{:S(2)}) copy-start(f32[128,64]{1,0:T(8,128)} %constant.59.clone.first_ref) | copy-start | bytes 98308
  0.0 26.2 %copy-start.4 = (f32[3,32,128]{2,1,0:T(8,128)S(1)}, f32[3,32,128]{2,1,0:T(8,128)}, u32[]{:S(2)}) copy-start(f32[3,32,128]{2,1,0:T(8,128)} %constant.58.clone.phase_ref) | copy-start | bytes 147460
  26.2 1.0 %copy-start = (f32[768,128]{1,0:T(8,128)S(1)}, f32[768,128]{1,0:T(8,128)}, u32[]{:S(2)}) copy-start(f32[768,128]{1,0:T(8,128)} %shard_map.82) | copy-start | bytes 1179652

commit v3 on v2

--- a/solution.py
+++ b/solution.py
@@ -181,9 +181,9 @@
 
 def sums_kernel(full_width, columns, slots, orders_ref, table_ref, packed_ref, out_ref, part_ref):
     step = pl.program_id(0)
-    block = table_ref.shape[1] // 8
-    quads = block // 4
-    first_slot = lax.axis_index("ma") * slots + step * block
+    quads = table_ref.shape[2] // 8
+    stride = slots // 4
+    first_slot = lax.axis_index("ma") * slots + step * quads
     first_column = lax.axis_index("ell") * columns
     sub_pair = lax.broadcasted_iota(jnp.int32, (8, LANES), 0) // 2
     lane8 = lax.broadcasted_iota(jnp.int32, (8, LANES), 1)
@@ -194,24 +194,38 @@
     inside = column < full_width - 1
 
     def one_quad(quad, carry):
-        base = pl.multiple_of(quad * 32, 32)
-        parts = [[], [], [], []]
+        eight = pl.ds(pl.multiple_of(quad * 8, 8), 8)
+        weights = []
         for g in range(4):
-            lower = orders_ref[first_slot + quad * 4 + g]
+            lower = orders_ref[first_slot + g * stride + quad]
             is_lower = column < full_width - 1 - lower
             is_upper = jnp.logical_and(jnp.logical_not(is_lower), inside)
             upper_sign = alternate * (2 * (lower % 2) - 1).astype(jnp.float32)
-            parts[0].append(jnp.where(is_lower, 1.0, 0.0))
-            parts[1].append(jnp.where(is_lower, alternate, 0.0))
-            parts[2].append(jnp.where(is_upper, 1.0, 0.0))
-            parts[3].append(jnp.where(is_upper, upper_sign, 0.0))
-        weights = [jnp.concatenate(p, axis=0).astype(jnp.bfloat16) for p in parts]
-        tables = [table_ref[t, pl.ds(base, 32), :] for t in range(3)]
-        first = pl.multiple_of(quad * 384, 32)
+            weights.append(
+                (
+                    jnp.where(is_lower, 1.0, 0.0),
+                    jnp.where(is_lower, alternate, 0.0),
+                    jnp.where(is_upper, 1.0, 0.0),
+                    jnp.where(is_upper, upper_sign, 0.0),
+                )
+            )
+
+        def weighted(kinds, members):
+            values = {
+                (t, g): table_ref[t, g, eight, :].astype(jnp.float32)
+                for t in kinds
+                for g in members
+            }
+            return jnp.concatenate(
+                [values[t, g] * weights[g][q] for t in kinds for q in range(4) for g in members],
+                axis=0,
+            ).astype(jnp.bfloat16)
+
+        first = pl.multiple_of(quad * 96, 32)
         where_to = pl.multiple_of((step * quads + quad) * 8, 8)
-        left = jnp.concatenate([tables[0] * w for w in weights], axis=0)
+        left = weighted((0,), range(4))
         right = jnp.concatenate(
-            [packed_ref[pl.ds(first + 96 * g, 32), :] for g in range(4)], axis=0
+            [packed_ref[g, pl.ds(first, 32), :] for g in range(4)], axis=0
         )
         product = lax.dot_general(left, right, NT, preferred_element_type=jnp.float32)
         group = []
@@ -224,16 +238,9 @@
             group.append(chosen)
         part_ref[0, pl.ds(where_to, 8), :] = rotate_sums(group, lane_tile, sub_pair)
         for p in range(2):
-            left = jnp.concatenate(
-                [
-                    tables[t][p * 16 : p * 16 + 16] * w[p * 16 : p * 16 + 16]
-                    for t in (1, 2)
-                    for w in weights
-                ],
-                axis=0,
-            )
+            left = weighted((1, 2), (2 * p, 2 * p + 1))
             right = jnp.concatenate(
-                [packed_ref[pl.ds(first + 96 * (2 * p + g) + 32, 64), :] for g in range(2)], axis=0
+                [packed_ref[2 * p + g, pl.ds(first + 32, 64), :] for g in range(2)], axis=0
             )
             product = lax.dot_general(left, right, NT, preferred_element_type=jnp.float32)
             for t in range(2):
@@ -294,28 +301,29 @@
     return part_ref.shape[1] // 8
 
 
-UNROLL = 2
+UNROLL = 16
+BLOCK = 64
 
 
 def table_sums(legendre, harmonics, slot_orders):
     slots, columns = harmonics.shape[0], harmonics.shape[-1]
     full_width = 2 * slot_orders.shape[0]
     tables = (
-        legendre.reshape(3, slots, 2, 4, LANES).transpose(0, 1, 3, 2, 4).reshape(3, slots * 8, LANES)
+        legendre.reshape(3, slots, 2, 4, LANES).transpose(0, 1, 3, 2, 4).reshape(3, 4, slots * 2, LANES)
     )
     packed = (
         harmonics.reshape(slots, 3, 2, 4, 4, LANES)
         .transpose(0, 1, 2, 4, 3, 5)
-        .reshape(slots * 96, LANES)
-    )
-    block = 32
+        .reshape(4, slots * 24, LANES)
+    )
+    block = BLOCK
     return pl.pallas_call(
         functools.partial(sums_kernel, full_width, columns, slots),
         grid=(slots // block,),
         in_specs=[
             pl.BlockSpec(memory_space=pltpu.SMEM),
-            pl.BlockSpec((3, block * 8, LANES), lambda i: (0, i, 0)),
-            pl.BlockSpec((block * 96, LANES), lambda i: (i, 0)),
+            pl.BlockSpec((3, 4, block * 2, LANES), lambda i: (0, 0, i, 0)),
+            pl.BlockSpec((4, block * 24, LANES), lambda i: (0, i, 0)),
         ],
         out_specs=pl.BlockSpec((768, LANES), lambda i: (0, 0)),
         out_shape=jax.ShapeDtypeStruct((768, LANES), jnp.float32),
@@ -329,7 +337,7 @@
 
 
 def synthesis_kernel(
-    scalars_ref, orders_ref, sums_ref, phase_ref, first_ref, twist_ref, last_ref, out_ref,
+    width, cycle_ref, orders_ref, sums_ref, phase_ref, first_ref, twist_ref, last_ref, out_ref,
     left_ref, right_ref, held_ref, pixel_ref, landed_ref, send_sem, recv_sem, pixel_send, pixel_recv
 ):
     highest = lax.Precision.HIGHEST
@@ -377,13 +385,17 @@
     tall_ids = lax.broadcasted_iota(jnp.int32, (tall, LANES), 0)
     lane_rows = lax.broadcasted_iota(jnp.int32, (LANES, LANES), 0)
 
+    def order_rows(owner):
+        lower = orders_ref[owner]
+        return jnp.concatenate([lower, width - 1 - lower], axis=0)
+
     def await_step(step, carry):
         exchange(step).wait()
         return carry
 
     for near in range(owners):
         owner = lax.rem(my_owner + owners - near, owners)
-        ordered = orders_ref[pl.ds(pl.multiple_of(owner * 8, 8), 8), :]
+        ordered = order_rows(owner)
         for k in range(8):
             j = near * 8 + k
             right_ref[:, j * LANES : (j + 1) * LANES] = jnp.where(
@@ -391,7 +403,7 @@
             ).astype(jnp.bfloat16)
     for near in range(owners):
         owner = lax.rem(my_owner + owners - near, owners)
-        ordered = orders_ref[pl.ds(pl.multiple_of(owner * 8, 8), 8), :]
+        ordered = order_rows(owner)
         lax.fori_loop(max(1, near * sources), (near + 1) * sources, await_step, 0)
         total = held_ref[owner * sources]
         for source in range(1, sources):
@@ -413,7 +425,7 @@
     placed = lax.dot_general(
         left_ref[...], right_ref[...], NT, preferred_element_type=jnp.float32
     )
-    shifted = scalars_ref[0] == 1
+    shifted = cycle_ref[lax.rem(my_owner, cycle_ref.shape[0])] % 2 == 1
     factor = phase_ref[2]
     cosine = jnp.where(shifted, phase_ref[0], factor)
     sine = jnp.where(shifted, phase_ref[1], 0.0)
@@ -438,7 +450,7 @@
             + placed[at + tall : at + 2 * tall]
             + placed[at + 2 * tall : at + 3 * tall]
         )
-        is_real = scalars_ref[1 + rr] == 0
+        is_real = (my_source * 3 + rr) // 4 % 2 == 0
         spectrum = jnp.concatenate(
             [
                 value * jnp.where(is_real, cosine, -sine),
@@ -503,12 +515,13 @@
     return [jnp.asarray(t, jnp.float32) for t in (phase, first, twist, last)]
 
 
-def synthesis(sums, orders, scalars, sources, orders_count):
+def synthesis(sums, slot_orders, cycle_index, owners, sources):
+    orders_count = 2 * slot_orders.shape[0]
     tall = orders_count // LANES
     vmem = pl.BlockSpec(memory_space=pltpu.VMEM)
     pixels = (sources, 24, LANES)
     return pl.pallas_call(
-        synthesis_kernel,
+        functools.partial(synthesis_kernel, orders_count),
         in_specs=[pl.BlockSpec(memory_space=pltpu.SMEM)] + [vmem] * 6,
         out_specs=vmem,
         out_shape=jax.ShapeDtypeStruct((12, 8, LANES), jnp.float32),
@@ -526,31 +539,15 @@
         compiler_params=pltpu.CompilerParams(
             vmem_limit_bytes=32 * 1024 * 1024, collective_id=0, has_side_effects=True
         ),
-    )(scalars, orders, sums, *synthesis_tables(orders_count))
-
-
-def slot_layout(slot_orders, owners):
-    full_width = 2 * slot_orders.shape[0]
-    lower = slot_orders.reshape(owners, LANES, 4).transpose(0, 2, 1)
-    return jnp.stack([lower, full_width - 1 - lower], axis=1).reshape(owners * 8, LANES)
+    )(cycle_index, slot_orders.reshape(owners, 4, LANES), sums, *synthesis_tables(orders_count))
 
 
 def packed_body(legendre, harmonics, slot_orders, cycle_index):
     owners = lax.axis_size("ma")
     sources = lax.axis_size("ell")
-    full_width = 2 * slot_orders.shape[0]
-    pairs = cycle_index.shape[0]
-    me, part = lax.axis_index("ma"), lax.axis_index("ell")
-    shift = cycle_index[me % pairs] % 2
-    row = part * 3 + jnp.arange(3, dtype=jnp.int32)
-    scalars = jnp.concatenate([shift[None], (row // 4) % 2])
     sums = table_sums(legendre, harmonics, slot_orders)
     maps = synthesis(
-        sums.reshape(owners * sources, 24, LANES),
-        slot_layout(slot_orders, owners),
-        scalars,
-        sources,
-        full_width,
+        sums.reshape(owners * sources, 24, LANES), slot_orders, cycle_index, owners, sources
     )
     return maps.reshape(1, 3, 4, 8 * LANES)
 

time: 55.9 us -> 43.5 us (0.78)
  Pallas kernels: 49.1 us -> 41.5 us
  local copies, waits for them, and re-layouts: 4.09 us -> 1.65 us
  between operations: 2.01 us -> 0.06 us
    pallas_call x1, Pallas kernels: 21.6 us -> 14.1 us  [table_sums(): pl.pallas_call(functools.partial(sums_kernel, full_width, columns, slots)...]
    dynamic_slice x1 -> x0, local copies, waits for them, and re-layouts: 1.29 us -> none  [packed_body(): shift = cycle_index[me % pairs] % 2]
    reshape x1 -> x0, local copies, waits for them, and re-layouts: 0.95 us -> none  [slot_layout(): lower = slot_orders.reshape(owners, LANES, 4).transpose(0, 2, 1)]
where the time goes in v3:
time: 43.5 us; the launch traced here: 43.2 us
  Pallas kernels  41.5 us (95%)
  local copies, waits for them, and re-layouts  1.65 us (4%)
    pallas_call x1, Pallas kernels, synthesis(): pl.pallas_call(functools.partial(synthesis_kernel, orders_count), in_spec...  27.4 us
    pallas_call x1, Pallas kernels, table_sums(): pl.pallas_call(functools.partial(sums_kernel, full_width, columns, slots)...  14.1 us
    unnamed x14, local copies, waits for them, and re-layouts  1.01 us

profile of v3, /device:TPU:0, one launch (start us, length us, event | category | flops | bytes accessed | tf_op | source)
XLA Modules:
  0.0 43.2 jit_solution(6268302058193553234)
XLA Ops:
  0.0 0.0 copy-start.1
  0.0 0.0 copy-start.2
  0.0 0.0 copy-start.3
  0.0 0.0 copy-start.4
  0.0 0.0 copy-start.5
  0.0 0.0 copy-start.6
  0.0 14.1 %shard_map.82 = f32[768,128]{1,0:T(8,128)} custom-call(s32[2048]{0:T(1024)} %orders_ref.1, bf16[3,4,1024,128]{3,2,1,0:T(8,128)(2,1)} %bitcast.15, bf16[4,12288,128]{2,1,0:T(8,128)(2,1)} %bitcast.14), custom_call_target="tpu_custom_call" | custom-call | tf_op jit(solution)/shard_map/pallas_call | solution.py:320
  14.1 0.0 copy-done.1
  14.1 0.0 copy-done.2
  14.1 0.0 copy-done.3
  14.1 0.0 copy-done.4
  14.1 0.0 copy-done.5
  14.1 0.0 copy-done.6
  14.2 0.0 copy-start
  14.2 1.0 %copy-done = f32[768,128]{1,0:T(8,128)S(1)} copy-done((f32[768,128]{1,0:T(8,128)S(1)}, f32[768,128]{1,0:T(8,128)}, u32[]{:S(2)}) %copy-start) | copy-done | bytes 393240
  15.2 27.4 %shard_map.83 = f32[12,8,128]{2,1,0:T(8,128)S(1)} custom-call(s32[2]{0:T(128)S(1)} %copy-done.6, s32[4,4,128]{2,1,0:T(4,128)S(1)} %bitcast.13, f32[32,24,128]{2,1,0:T(8,128)S(1)} %bitcast.12, f32[3,32,128]{2,1,0:T(8,128)S(1)} %copy-done.4, f32[128,64]{1,0:T(8,128)S(1)} %copy-done.3, f32[2,64,128]{2,1,0:T(8,128)S(1)} %copy-done.2, f32[128,256]{1,0:T(8,128)S(1)} %copy-done.1), custom_call_target="tpu_custom_call" | custom-call | tf_op jit(solution)/shard_map/pallas_call | solution.py:523
  42.6 0.6 %reshape.27 = f32[1,3,4,1024]{3,2,1,0:T(4,128)} reshape(f32[12,8,128]{2,1,0:T(8,128)S(1)} %shard_map.83) | data formatting | bytes 98304 | tf_op jit(solution)/shard_map/reshape | solution.py:552
Async XLA Ops:
  0.0 14.1 %copy-start.1 = (f32[128,256]{1,0:T(8,128)S(1)}, f32[128,256]{1,0:T(8,128)}, u32[]{:S(2)}) copy-start(f32[128,256]{1,0:T(8,128)} %constant.11.clone.last_ref) | copy-start | bytes 393220
  0.0 14.1 %copy-start.2 = (f32[2,64,128]{2,1,0:T(8,128)S(1)}, f32[2,64,128]{2,1,0:T(8,128)}, u32[]{:S(2)}) copy-start(f32[2,64,128]{2,1,0:T(8,128)} %constant.10.clone.twist_ref) | copy-start | bytes 196612
  0.0 14.1 %copy-start.3 = (f32[128,64]{1,0:T(8,128)S(1)}, f32[128,64]{1,0:T(8,128)}, u32[]{:S(2)}) copy-start(f32[128,64]{1,0:T(8,128)} %constant.9.clone.first_ref) | copy-start | bytes 98308
  0.0 14.1 %copy-start.4 = (f32[3,32,128]{2,1,0:T(8,128)S(1)}, f32[3,32,128]{2,1,0:T(8,128)}, u32[]{:S(2)}) copy-start(f32[3,32,128]{2,1,0:T(8,128)} %constant.8.clone.phase_ref) | copy-start | bytes 147460
  0.0 14.1 %copy-start.5 = (s32[2048]{0:T(1024)S(1)}, s32[2048]{0:T(1024)}, u32[]{:S(2)}) copy-start(s32[2048]{0:T(1024)} %orders_ref.1) | copy-start | bytes 24580
  0.0 14.1 %copy-start.6 = (s32[2]{0:T(128)S(1)}, s32[2]{0:T(128)}, u32[]{:S(2)}) copy-start(s32[2]{0:T(128)} %cycle_ref.1) | copy-start | bytes 28
  14.2 1.0 %copy-start = (f32[768,128]{1,0:T(8,128)S(1)}, f32[768,128]{1,0:T(8,128)}, u32[]{:S(2)}) copy-start(f32[768,128]{1,0:T(8,128)} %shard_map.82) | copy-start | bytes 1179652
